TPU v7x, 32 devices: a whole 2x2x4 slice. The times are simulated.
32 devices in a mesh: row: 8 (over y, x, core), col: 4 (over z).
Axes of the slice: x: 2, y: 2, z: 4, core: 2. Of those that a mesh axis runs over, the one named last changes fastest.
Arguments:
- samples: float32 [32768, 32], P(('row', 'col')), may hold values from -3 to 3
- sample_logw: float32 [32768], P(('row', 'col')), may hold values from -8 to 8
- references: float32 [65536, 32], P(('row', 'col')), may hold values from -3 to 3
- reference_logw: float32 [65536], P(('row', 'col')), may hold values from -8 to 8
- dual_start: float32 [8, 4096], P('row'), may hold values from -3 to 3
- kept_tiles: int32 [8, 4, 32], P('row', 'col'), may hold values from 0 to 255, as said below
- tile_counts: int32 [8, 4], P('row', 'col'), may hold values from 4 to 32, as said below
Outputs:
- row_duals: float32 [8, 4096], P('row')
- col_duals: float32 [4, 16384], P('col')
Inputs may be any that keep to these rules, and one draw needn't show every extreme that they name: `kept_tiles`: on device (i, j) the first tile_counts[i, j] entries are distinct tiles r * 32 + c of its 8 by 32 grid; later entries are tiles of that grid and unused. Every block of every sample group and of every reference group lies in some used tile. `tile_counts`: 32 on at least one device.
All inputs are finite; a program needn't handle non-finite values.
Results may differ from a plain program's by a relative error of at most 0.0003.
Values sent between devices are 32-bit elements; how exact they have to be, the bound alone decides.
No kernel may reach another device: no remote copies, remote signals or barrier semaphores. Data moves between devices by JAX's collectives and lax.ppermute only.
A program may use at most 64 MiB of HBM per device.

v0:
```python
import functools
import math

import jax
import jax.numpy as jnp
from jax import lax
from jax.experimental import pallas as pl
from jax.experimental.pallas import tpu as pltpu
from jax.sharding import PartitionSpec as P


TILE = 512
ITERS = 3
LANES = 128
BIAS = 16
SHIFT = 12
CODE = 1 << SHIFT
UNROLL = 8
SAMPLE = 128
MARGIN = 80.0

lowest = -1e30
epsilon = 0.1
log2e = math.log2(math.e)
ln2 = math.log(2.0)


VM = pl.BlockSpec(memory_space=pltpu.VMEM)
HBM = pl.BlockSpec(memory_space=pltpu.HBM)
SM = pl.BlockSpec(memory_space=pltpu.SMEM)
PARAMS = pltpu.CompilerParams(vmem_limit_bytes=24 * 1024 * 1024)


def swap(value, axis, distance):
    pairs = [(i, i ^ distance) for i in range(lax.axis_size(axis))]
    return jax.tree.map(lambda part: lax.ppermute(part, axis, pairs), value)


def pack_kernel(xt_ref, wx_hbm, yt_ref, wy_hbm, *refs):
    *outs, wx_ref, wy_ref, sem = refs
    dim = xt_ref.shape[0]
    chunks = TILE // LANES
    copies = [(wx_hbm, wx_ref), (wy_hbm, wy_ref)]
    stores = []

    def put(out, b, points_ref, weights_ref, block):
        start = pl.multiple_of(block * TILE, TILE)
        for j in range(chunks):
            source = points_ref.at[:, pl.ds(start + j * LANES, LANES)]
            copies.append((source, out.at[b, pl.ds(j * dim, dim), :]))
        stores.append((out, b, weights_ref, block))

    x_ref, keep_ref, *send_refs = outs
    for b in range(x_ref.shape[0]):
        put(x_ref, b, xt_ref, wx_ref, b)
    if send_refs:
        parity = lax.rem(lax.axis_index("row"), 2)
        for b in range(keep_ref.shape[0]):
            put(send_refs[0], b, yt_ref, wy_ref, 2 * b + 1 - parity)
        for b in range(keep_ref.shape[0]):
            put(keep_ref, b, yt_ref, wy_ref, 2 * b + parity)
    else:
        for b in range(keep_ref.shape[0]):
            put(keep_ref, b, yt_ref, wy_ref, b)
    started = [pltpu.make_async_copy(a, b, sem.at[i]) for i, (a, b) in enumerate(copies)]
    for copy in started:
        copy.start()
    for copy in started[:2]:
        copy.wait()
    for out, b, weights_ref, block in stores:
        out[b, chunks * dim : chunks * (dim + 1), :] = weights_ref[pl.ds(block * chunks, chunks), :]
    for copy in started[2:]:
        copy.wait()


def collect_tiles(tiles_own, tiles_partner, row_blocks, col_blocks):
    slots = tiles_own.shape[0] - 1

    def kernel(t_own, t_partner, found):
        parity = lax.rem(lax.axis_index("row"), 2)

        def collect(ref, side, filled):
            def visit(k, filled):
                tile = ref[k]
                r, c = lax.div(tile, col_blocks), lax.rem(tile, col_blocks)
                found[filled] = (side * row_blocks + r) * CODE + lax.div(c, 2)
                return filled + (lax.rem(c, 2) == parity).astype(jnp.int32)

            return lax.fori_loop(0, ref[slots], visit, filled)

        filled = collect(t_own, parity, jnp.int32(1))
        filled = collect(t_partner, 1 - parity, filled)
        found[0] = filled - 1
        found[filled] = 0

    return pl.pallas_call(
        kernel,
        out_shape=jax.ShapeDtypeStruct((2 * slots + 2,), jnp.int32),
        in_specs=[SM] * 2,
        out_specs=SM,
        compiler_params=PARAMS,
        name="collect",
    )(tiles_own, tiles_partner)


def prepare(own_x, partner_x, own_y, partner_y, dual_own, dual_partner, sizes):
    row_blocks, col_blocks, dim = sizes
    n_x, n_y = len(own_x), len(own_y)
    both = len(partner_y) > 0
    per_x = own_x[0].shape[0]
    per_y = own_y[0].shape[0] * (2 if both else 1)
    half_cols = col_blocks // 2
    all_rows = 2 * row_blocks
    chunks = TILE // LANES

    def kernel(*refs):
        refs = list(refs)

        def take(n):
            out = refs[:n]
            del refs[:n]
            return out

        xs, pxs, ys, pys = take(n_x), take(n_x), take(n_y), take(len(partner_y))
        d_own, d_partner = take(2)
        xp, yp, u0, wx, wy, nx, ny = take(7)
        row, col = lax.axis_index("row"), lax.axis_index("col")
        parity = lax.rem(row, 2)
        pair = lax.div(row, 2)

        def load(ref, b):
            points = jnp.concatenate([ref[b, j * dim : (j + 1) * dim, :] for j in range(chunks)], axis=1)
            base = chunks * dim
            weights = jnp.concatenate([ref[b, base + j : base + j + 1, :] for j in range(chunks)], axis=1)
            return points, weights

        def split(out, index, points):
            high = points.astype(jnp.bfloat16)
            low = (points - high.astype(jnp.float32)).astype(jnp.bfloat16)
            out[index, 0:dim, :] = high
            out[index, dim : 2 * dim, :] = low

        for group, (sources, duals) in enumerate(((xs, d_own), (pxs, d_partner))):
            side = parity if group == 0 else 1 - parity
            for d in range(n_x):
                for b in range(per_x):
                    local = (col ^ d) * per_x + b
                    index = side * row_blocks + local
                    points, weights = load(sources[d], b)
                    norm = jnp.sum(points * points, axis=0, keepdims=True)
                    split(xp, index, points * (2.0 * log2e / epsilon))
                    start = pl.multiple_of(local * TILE, TILE)
                    dual = duals[0:1, pl.ds(start, TILE)]
                    u0[pl.ds(index, 1), :] = log2e * weights + (dual - norm) * (log2e / epsilon)
                    wx[pl.ds(index, 1), :] = log2e * weights
                    nx[pl.ds(index, 1), :] = norm
        for d in range(n_y):
            place = pair ^ d
            for from_partner in range(2 if both else 1):
                source = (ys, pys)[from_partner][d]
                here = source.shape[0]
                for b in range(here):
                    index = place * per_y + b
                    if both:
                        index = index + (parity if from_partner == 0 else 1 - parity) * here
                    points, weights = load(source, b)
                    norm = jnp.sum(points * points, axis=0, keepdims=True)
                    split(yp, index, points)
                    wy[pl.ds(index, 1), :] = log2e * weights
                    ny[pl.ds(index, 1), :] = norm

    f32, bf16 = jnp.float32, jnp.bfloat16
    shape = jax.ShapeDtypeStruct
    rows, cols = (all_rows, TILE), (half_cols, TILE)
    return pl.pallas_call(
        kernel,
        out_shape=(
            shape((all_rows, 2 * dim, TILE), bf16),
            shape((half_cols, 2 * dim, TILE), bf16),
            shape(rows, f32),
            shape(rows, f32),
            shape(cols, f32),
            shape(rows, f32),
            shape(cols, f32),
        ),
        in_specs=[VM] * (2 * n_x + n_y + len(partner_y) + 2),
        out_specs=(VM,) * 7,
        compiler_params=PARAMS,
        name="prepare",
    )(*own_x, *partner_x, *own_y, *partner_y, dual_own, dual_partner)


def log_sum(parts):
    if len(parts) == 1:
        return parts[0]
    peak = functools.reduce(jnp.maximum, parts)
    total = functools.reduce(jnp.add, [jnp.exp2(part - peak) for part in parts])
    return peak + jnp.log2(total)


def half_step(from_points, to_points, weights, parts, guess, tiles, from_first, keep_total):
    m_blocks, width, _ = from_points.shape
    n_blocks = to_points.shape[0]
    dim = width // 2
    n_parts = len(parts)
    groups = TILE // 8
    guessed = guess is not None

    def kernel(*refs):
        tiles_ref, a_ref, b_ref, w_ref = refs[:4]
        part_refs = refs[4 : 4 + n_parts]
        rest = list(refs[4 + n_parts :])
        guess_ref = rest.pop(0) if guessed else None
        out_ref = rest.pop(0)
        total_ref = rest.pop(0) if keep_total else None
        lifts, drops, peaks, sums, s0, s1, p0, p1 = rest
        n = tiles_ref[0]

        def ends(k):
            code = tiles_ref[jnp.minimum(k, n) + 1]
            first, second = lax.shift_right_logical(code, SHIFT), code & (CODE - 1)
            return (first, second) if from_first else (second, first)


        if n_parts:
            total = log_sum([ref[...] for ref in part_refs])
            if keep_total:
                total_ref[...] = total
            lift = w_ref[...] - total
        else:
            lift = w_ref[...]
        place = lax.broadcasted_iota(jnp.int32, (BIAS, TILE), 0)

        def pieces(out, value, first, ones):
            high = value.astype(jnp.bfloat16).astype(jnp.float32)
            rest = value - high
            middle = rest.astype(jnp.bfloat16).astype(jnp.float32)
            low = rest - middle
            filler = jnp.where((place >= ones) & (place < ones + 3), 1.0, 0.0)
            for i in range(value.shape[0]):
                rows = filler
                for at, part in enumerate((high, middle, low)):
                    rows = jnp.where(place == first + at, part[i : i + 1, :], rows)
                out[i] = rows.astype(jnp.bfloat16)

        pieces(lifts, lift, 0, 3)
        plain = jnp.where(place < 3, 1.0, 0.0).astype(jnp.bfloat16)

        def doubled(ref, i, high_first):
            both = ref[i]
            if high_first:
                return [both[0:dim], both]
            return [both, both[0:dim]]

        def product(k, shifted, rows=TILE):
            m, c = ends(k)
            left = jnp.concatenate(doubled(a_ref, m, not from_first) + [lifts[m]], axis=0)[:, :rows]
            right = jnp.concatenate(doubled(b_ref, c, from_first) + [drops[c] if shifted else plain], axis=0)
            value = lax.dot_general(left, right, (((0,), (0,)), ((), ())), preferred_element_type=jnp.float32)
            return value.reshape(rows // 8, 8, TILE)

        def target(k):
            return jnp.where(k < n, ends(k)[1], n_blocks)

        def exact():
            peaks[...] = jnp.full(peaks.shape, lowest, jnp.float32)
            sums[...] = jnp.zeros(sums.shape, jnp.float32)

            def scores(k, score, peak):
                value = product(k, False)
                score[...] = value
                peak[...] = jnp.max(value, axis=0)

            def absorb(k, score, peak):
                c = target(k)
                before = peaks[c]
                after = jnp.maximum(before, peak[...])
                total = jnp.sum(jnp.exp2(score[...] - after[None]), axis=0)
                sums[c] = sums[c] * jnp.exp2(before - after) + total
                peaks[c] = after

            scores(0, s0, p0)

            def visit(step, carry):
                scores(2 * step + 1, s1, p1)
                absorb(2 * step, s0, p0)
                scores(2 * step + 2, s0, p0)
                absorb(2 * step + 1, s1, p1)
                return carry

            lax.fori_loop(0, lax.div(n + 1, 2), visit, 0)
            top = peaks[0:n_blocks]
            peak = jnp.max(top, axis=1)
            total = jnp.sum(sums[0:n_blocks] * jnp.exp2(top - peak[:, None, :]), axis=1)
            out_ref[...] = jnp.where(total > 0.0, peak + jnp.log2(total), lowest)

        batches = lax.div(n + UNROLL - 1, UNROLL)
        if guessed:
            shift = guess_ref[...]
        else:
            peaks[...] = jnp.full(peaks.shape, lowest, jnp.float32)

            def look(step, carry):
                found = []
                for u in range(UNROLL):
                    k = UNROLL * step + u
                    found.append((target(k), jnp.max(product(k, False, SAMPLE), axis=0)))
                for c, peak in found:
                    peaks[c] = jnp.maximum(peaks[c], peak)
                return carry

            lax.fori_loop(0, batches, look, 0)
            shift = jnp.max(peaks[0:n_blocks], axis=1) + MARGIN
        used = shift > 0.5 * lowest
        shift = jnp.where(used, shift, 0.0)
        pieces(drops, -shift, 3, 0)
        sums[...] = jnp.zeros(sums.shape, jnp.float32)

        def batch(start, size):
            found = []
            for k in range(size):
                value = product(start + k, True)
                found.append((target(start + k), jnp.sum(jnp.exp2(value), axis=0)))
            for c, total in found:
                sums[c] += total

        def visit(step, carry):
            batch(UNROLL * step, UNROLL)
            return carry

        even = lax.div(n + 1, 2) * 2
        full = lax.div(even, UNROLL)
        lax.fori_loop(0, full, visit, 0)
        done = full * UNROLL
        size = UNROLL // 2
        while size > 1:
            fits = even - done >= size
            pl.when(fits)(functools.partial(batch, done, size))
            done = jnp.where(fits, done + size, done)
            size //= 2
        total = jnp.sum(sums[0:n_blocks], axis=1)
        out_ref[...] = jnp.where(used, shift + jnp.log2(total), lowest)
        inside = (total > 2.0**-90) & (total < 2.0**120)
        outside = jnp.max(jnp.where(used & ~inside, 1.0, 0.0))
        pl.when(outside > 0.5)(exact)

    f32 = jnp.float32
    shape = jax.ShapeDtypeStruct
    out_shape = [shape((n_blocks, TILE), f32)] + ([shape((m_blocks, TILE), f32)] if keep_total else [])
    extra = (guess,) if guessed else ()
    return pl.pallas_call(
        kernel,
        out_shape=out_shape,
        in_specs=[SM] + [VM] * (3 + n_parts + len(extra)),
        out_specs=[VM] * len(out_shape),
        scratch_shapes=[
            pltpu.VMEM((m_blocks, BIAS, TILE), jnp.bfloat16),
            pltpu.VMEM((n_blocks, BIAS, TILE), jnp.bfloat16),
            pltpu.VMEM((n_blocks + 1, 8, TILE), f32),
            pltpu.VMEM((n_blocks + 1, 8, TILE), f32),
            pltpu.VMEM((groups, 8, TILE), f32),
            pltpu.VMEM((groups, 8, TILE), f32),
            pltpu.VMEM((8, TILE), f32),
            pltpu.VMEM((8, TILE), f32),
        ],
        compiler_params=PARAMS,
        name="column_step" if from_first else "row_step",
    )(tiles, from_points, to_points, weights, *parts, *extra)


def per_device(samples, sample_logw, references, reference_logw, dual_start, kept_tiles, tile_counts):
    n_row, n_col = lax.axis_size("row"), lax.axis_size("col")
    dim = samples.shape[1]
    own_row_blocks = samples.shape[0] // TILE
    own_col_blocks = references.shape[0] // TILE
    row_blocks, col_blocks = own_row_blocks * n_col, own_col_blocks * n_row
    chunks = TILE // LANES
    parity = lax.axis_index("row") % 2
    both = own_col_blocks % 2 == 0
    assert both or own_col_blocks == 1

    shape = jax.ShapeDtypeStruct
    depth = chunks * (dim + 1)
    kept = own_col_blocks // 2 if both else own_col_blocks
    packed_shapes = [shape((own_row_blocks, depth, LANES), jnp.float32)]
    packed_shapes += [shape((kept, depth, LANES), jnp.float32)] * (2 if both else 1)
    packed = pl.pallas_call(
        pack_kernel,
        out_shape=packed_shapes,
        in_specs=[HBM] * 4,
        out_specs=[VM] * len(packed_shapes),
        scratch_shapes=[
            pltpu.VMEM((own_row_blocks * chunks, LANES), jnp.float32),
            pltpu.VMEM((own_col_blocks * chunks, LANES), jnp.float32),
            pltpu.SemaphoreType.DMA((chunks * (own_row_blocks + own_col_blocks) + 2,)),
        ],
        compiler_params=PARAMS,
        name="pack",
    )(
        samples.T,
        sample_logw.reshape(-1, LANES),
        references.T,
        reference_logw.reshape(-1, LANES),
    )
    x_pack, y_keep = packed[0], packed[1]
    sends = [("col", d, x_pack) for d in range(n_col - 1, 0, -1)]
    plane = [("row", 2 * d, y_keep) for d in range(n_row // 2 - 1, 0, -1)]
    if both:
        plane += [("row", 2 * d + 1, packed[2]) for d in range(n_row // 2 - 1, -1, -1)]
    pace = max(1, len(plane) // len(sends))
    order = []
    while sends or plane:
        order += sends[:1] + plane[:pace]
        sends, plane = sends[1:], plane[pace:]
    tiles_own = jnp.concatenate([kept_tiles[0, 0], tile_counts[0]])
    order[2:2] = [("row", 0, tiles_own), ("row", -1, dual_start)]
    got = {}
    for axis, distance, value in order:
        got[axis, distance] = swap(value, axis, distance if distance > 0 else 1)
    own_y = [y_keep] + [got["row", 2 * d] for d in range(1, n_row // 2)]
    partner_y = [got["row", 2 * d + 1] for d in range(n_row // 2)] if both else []
    own_x = [x_pack] + [got["col", d] for d in range(1, n_col)]
    partner_x = [swap(part, "row", 1) for part in own_x]
    tiles_partner, dual_partner = got["row", 0], got["row", -1]
    tiles = collect_tiles(tiles_own, tiles_partner, row_blocks, col_blocks)
    xp, yp, start, wx, wy, nx, ny = prepare(
        own_x, partner_x, own_y, partner_y, dual_start, dual_partner, (row_blocks, col_blocks, dim)
    )

    row_parts = []
    col_guess = row_guess = None
    for turn in range(ITERS):
        last = turn == ITERS - 1
        (part,) = half_step(xp, yp, wx if turn else start, row_parts, col_guess, tiles, True, False)
        col_guess = part
        col_parts = [part] + [swap(part, "row", 2 * d) for d in range(1, n_row // 2)]
        part, *kept_total = half_step(yp, xp, wy, col_parts, row_guess, tiles, False, last)
        row_guess = part
        part = log_sum([part, swap(part, "row", 1)])
        row_parts = [part] + [swap(part, "col", d) for d in range(1, n_col)]

    own = [lax.dynamic_slice_in_dim(part, parity * row_blocks, row_blocks, 0) for part in row_parts]
    norms = lax.dynamic_slice_in_dim(nx, parity * row_blocks, row_blocks, 0)
    row_duals = norms - (epsilon * ln2) * log_sum(own)
    col_half = ny - (epsilon * ln2) * kept_total[0]
    col_other = swap(col_half, "row", 1)
    even = jnp.where(parity == 0, col_half, col_other)
    odd = jnp.where(parity == 0, col_other, col_half)
    col_duals = jnp.stack([even, odd], axis=1)
    return (row_duals.reshape(1, -1), col_duals.reshape(1, -1))


def solution(mesh):
    return jax.shard_map(
        per_device,
        mesh=mesh,
        in_specs=(
            P(("row", "col"), None),
            P(("row", "col")),
            P(("row", "col"), None),
            P(("row", "col")),
            P("row", None),
            P("row", "col", None),
            P("row", "col"),
        ),
        out_specs=(P("row", None), P("col", None)),
        check_vma=False,
    )
```

profile of v0, /device:TPU:0, one launch (start us, length us, event | category | flops | bytes accessed | tf_op | source)
XLA Modules:
  0.0 133.4 jit_solution(8726922217709965881)
XLA Ops:
  4.3 3.1 %collective-permute-start = (f32[2,132,128]{2,1,0:T(8,128)S(1)}, f32[2,132,128]{2,1,0:T(8,128)S(1)}, u32[]{:S(2)}, u32[]{:S(2)}) collective-permute-start(f32[2,132,128]{2,1,0:T(8,128)S(1)} %get-tuple-element.14.refs_0_), channel_id=1, source_target_pairs={{0,1},{1,0},{2,3},{3,2},{4,5},{5,4},{6,7},{7,6},{8,9},{9,8},{10,11... | collective-permute-start | bytes 405512 | tf_op jit(solution)/shard_map/ppermute | solution.py:36
  7.4 2.6 %collective-permute-start.1 = (f32[2,132,128]{2,1,0:T(8,128)S(1)}, f32[2,132,128]{2,1,0:T(8,128)S(1)}, u32[]{:S(2)}, u32[]{:S(2)}) collective-permute-start(f32[2,132,128]{2,1,0:T(8,128)S(1)} %get-tuple-element.14.refs_0_), channel_id=1, source_target_pairs={{0,2},{1,3},{2,0},{3,1},{4,6},{5,7},{6,4},{7,5},{8,10},{9,11},{10,... | collective-permute-start | bytes 405512 | tf_op jit(solution)/shard_map/ppermute | solution.py:36
  15.7 5.1 %collective-permute-done.1.refs_2_ = f32[2,132,128]{2,1,0:T(8,128)S(1)} collective-permute-done((f32[2,132,128]{2,1,0:T(8,128)S(1)}, f32[2,132,128]{2,1,0:T(8,128)S(1)}, u32[]{:S(2)}, u32[]{:S(2)}) %collective-permute-start.1) | collective-permute-done | bytes 135200 | tf_op jit(solution)/shard_map/ppermute | solution.py:36
  20.8 2.7 %collective-permute-start.13 = (f32[2,132,128]{2,1,0:T(8,128)S(1)}, f32[2,132,128]{2,1,0:T(8,128)S(1)}, u32[]{:S(2)}, u32[]{:S(2)}) collective-permute-start(f32[2,132,128]{2,1,0:T(8,128)S(1)} %get-tuple-element.16), channel_id=1, source_target_pairs={{0,28},{4,24},{8,20},{12,16},{16,12},{20,8},{24,4},{28,0},{1,29},{... | collective-permute-start | bytes 405512 | tf_op jit(solution)/shard_map/ppermute | solution.py:36
  27.0 3.4 %collective-permute-done.12.refs_14_ = f32[2,132,128]{2,1,0:T(8,128)S(1)} collective-permute-done((f32[2,132,128]{2,1,0:T(8,128)S(1)}, f32[2,132,128]{2,1,0:T(8,128)S(1)}, u32[]{:S(2)}, u32[]{:S(2)}) %collective-permute-start.12) | collective-permute-done | bytes 135200 | tf_op jit(solution)/shard_map/ppermute | solution.py:36
  33.2 2.6 %collective-permute-done.8.refs_10_ = f32[2,132,128]{2,1,0:T(8,128)S(1)} collective-permute-done((f32[2,132,128]{2,1,0:T(8,128)S(1)}, f32[2,132,128]{2,1,0:T(8,128)S(1)}, u32[]{:S(2)}, u32[]{:S(2)}) %collective-permute-start.8) | collective-permute-done | bytes 135200 | tf_op jit(solution)/shard_map/ppermute | solution.py:36
  36.6 6.4 %column_step.3.refs_4_.refs_8_ = f32[16,512]{1,0:T(8,128)S(1)} custom-call(s32[66]{0:T(128)S(1)} %collect.1.refs_0_, bf16[16,64,512]{2,1,0:T(8,128)(2,1)S(1)} %get-tuple-element.19.refs_1_.refs_2_, bf16[16,64,512]{2,1,0:T(8,128)(2,1)S(1)} %get-tuple-element.18.refs_2_.refs_1_, f32[16,512]{1,0:T(8,128)S(1)} %get-tuple-element.22.refs_3_), custom_call_target="tpu_custom_call" | custom-call | tf_op jit(solution)/shard_map/column_step/pallas_call | solution.py:351
  43.6 3.0 %collective-permute-start.18 = (f32[16,512]{1,0:T(8,128)S(1)}, f32[16,512]{1,0:T(8,128)S(1)}, u32[]{:S(2)}, u32[]{:S(2)}) collective-permute-start(f32[16,512]{1,0:T(8,128)S(1)} %column_step.3.refs_4_.refs_8_), channel_id=1, source_target_pairs={{0,24},{4,28},{8,16},{12,20},{16,8},{20,12},{24,0},{28,4},{1,25},{... | collective-permute-start | bytes 98312 | tf_op jit(solution)/shard_map/ppermute | solution.py:36
  48.4 14.5 %row_step.3.refs_8_ = f32[16,512]{1,0:T(8,128)S(1)} custom-call(s32[66]{0:T(128)S(1)} %collect.1.refs_0_, bf16[16,64,512]{2,1,0:T(8,128)(2,1)S(1)} %get-tuple-element.18.refs_2_.refs_1_, bf16[16,64,512]{2,1,0:T(8,128)(2,1)S(1)} %get-tuple-element.19.refs_1_.refs_2_, f32[16,512]{1,0:T(8,128)S(1)} %get-tuple-element.20.refs_3_, ...), custom_call_target="tpu_custom_call" | custom-call | tf_op jit(solution)/shard_map/row_step/pallas_call | solution.py:351
  64.3 2.6 %collective-permute-start.20 = (f32[16,512]{1,0:T(8,128)S(1)}, f32[16,512]{1,0:T(8,128)S(1)}, u32[]{:S(2)}, u32[]{:S(2)}) collective-permute-start(f32[16,512]{1,0:T(8,128)S(1)} %multiply_add_fusion.2.refs_4_), channel_id=1, source_target_pairs={{0,1},{1,0},{2,3},{3,2},{4,5},{5,4},{6,7},{7,6},{8,9},{9,8},{10,11... | collective-permute-start | bytes 98312 | tf_op jit(solution)/shard_map/ppermute | solution.py:36
  66.9 4.3 %collective-permute-start.21 = (f32[16,512]{1,0:T(8,128)S(1)}, f32[16,512]{1,0:T(8,128)S(1)}, u32[]{:S(2)}, u32[]{:S(2)}) collective-permute-start(f32[16,512]{1,0:T(8,128)S(1)} %multiply_add_fusion.2.refs_4_), channel_id=1, source_target_pairs={{0,2},{1,3},{2,0},{3,1},{4,6},{5,7},{6,4},{7,5},{8,10},{9,11},{10,... | collective-permute-start | bytes 98312 | tf_op jit(solution)/shard_map/ppermute | solution.py:36
  71.2 2.5 %collective-permute-done.21.refs_6_ = f32[16,512]{1,0:T(8,128)S(1)} collective-permute-done((f32[16,512]{1,0:T(8,128)S(1)}, f32[16,512]{1,0:T(8,128)S(1)}, u32[]{:S(2)}, u32[]{:S(2)}) %collective-permute-start.21) | collective-permute-done | bytes 32800 | tf_op jit(solution)/shard_map/ppermute | solution.py:36
  73.7 3.2 %collective-permute-done.22.refs_7_ = f32[16,512]{1,0:T(8,128)S(1)} collective-permute-done((f32[16,512]{1,0:T(8,128)S(1)}, f32[16,512]{1,0:T(8,128)S(1)}, u32[]{:S(2)}, u32[]{:S(2)}) %collective-permute-start.22) | collective-permute-done | bytes 32800 | tf_op jit(solution)/shard_map/ppermute | solution.py:36
  76.9 5.1 %column_step.4.refs_4_.refs_8_ = f32[16,512]{1,0:T(8,128)S(1)} custom-call(s32[66]{0:T(128)S(1)} %collect.1.refs_0_, bf16[16,64,512]{2,1,0:T(8,128)(2,1)S(1)} %get-tuple-element.19.refs_1_.refs_2_, bf16[16,64,512]{2,1,0:T(8,128)(2,1)S(1)} %get-tuple-element.18.refs_2_.refs_1_, f32[16,512]{1,0:T(8,128)S(1)} %get-tuple-element.21.refs_3_, ...), custom_call_target="tpu_custom_call" | custom-call | tf_op jit(solution)/shard_map/column_step/pallas_call | solution.py:351
  82.1 7.7 %collective-permute-start.24 = (f32[16,512]{1,0:T(8,128)S(1)}, f32[16,512]{1,0:T(8,128)S(1)}, u32[]{:S(2)}, u32[]{:S(2)}) collective-permute-start(f32[16,512]{1,0:T(8,128)S(1)} %column_step.4.refs_4_.refs_8_), channel_id=1, source_target_pairs={{0,16},{4,20},{8,24},{12,28},{16,0},{20,4},{24,8},{28,12},{1,17},{... | collective-permute-start | bytes 98312 | tf_op jit(solution)/shard_map/ppermute | solution.py:36
  89.9 1.9 %collective-permute-done.24.refs_6_ = f32[16,512]{1,0:T(8,128)S(1)} collective-permute-done((f32[16,512]{1,0:T(8,128)S(1)}, f32[16,512]{1,0:T(8,128)S(1)}, u32[]{:S(2)}, u32[]{:S(2)}) %collective-permute-start.24) | collective-permute-done | bytes 32800 | tf_op jit(solution)/shard_map/ppermute | solution.py:36
  91.8 2.9 %collective-permute-done.25.refs_7_ = f32[16,512]{1,0:T(8,128)S(1)} collective-permute-done((f32[16,512]{1,0:T(8,128)S(1)}, f32[16,512]{1,0:T(8,128)S(1)}, u32[]{:S(2)}, u32[]{:S(2)}) %collective-permute-start.25) | collective-permute-done | bytes 32800 | tf_op jit(solution)/shard_map/ppermute | solution.py:36
  94.7 4.9 %row_step.4.refs_8_ = f32[16,512]{1,0:T(8,128)S(1)} custom-call(s32[66]{0:T(128)S(1)} %collect.1.refs_0_, bf16[16,64,512]{2,1,0:T(8,128)(2,1)S(1)} %get-tuple-element.18.refs_2_.refs_1_, bf16[16,64,512]{2,1,0:T(8,128)(2,1)S(1)} %get-tuple-element.19.refs_1_.refs_2_, f32[16,512]{1,0:T(8,128)S(1)} %get-tuple-element.20.refs_3_, ...), custom_call_target="tpu_custom_call" | custom-call | tf_op jit(solution)/shard_map/row_step/pallas_call | solution.py:351
  101.1 4.3 %collective-permute-start.29 = (f32[16,512]{1,0:T(8,128)S(1)}, f32[16,512]{1,0:T(8,128)S(1)}, u32[]{:S(2)}, u32[]{:S(2)}) collective-permute-start(f32[16,512]{1,0:T(8,128)S(1)} %multiply_add_fusion.1.refs_4_), channel_id=1, source_target_pairs={{0,3},{1,2},{2,1},{3,0},{4,7},{5,6},{6,5},{7,4},{8,11},{9,10},{10,... | collective-permute-start | bytes 98312 | tf_op jit(solution)/shard_map/ppermute | solution.py:36
  107.6 4.9 %column_step.5.refs_4_ = f32[16,512]{1,0:T(8,128)S(1)} custom-call(s32[66]{0:T(128)S(1)} %collect.1.refs_0_, bf16[16,64,512]{2,1,0:T(8,128)(2,1)S(1)} %get-tuple-element.19.refs_1_.refs_2_, bf16[16,64,512]{2,1,0:T(8,128)(2,1)S(1)} %get-tuple-element.18.refs_2_.refs_1_, f32[16,512]{1,0:T(8,128)S(1)} %get-tuple-element.21.refs_3_, ...), custom_call_target="tpu_custom_call" | custom-call | tf_op jit(solution)/shard_map/column_step/pallas_call | solution.py:351
  112.7 3.4 %collective-permute-start.32 = (f32[16,512]{1,0:T(8,128)S(1)}, f32[16,512]{1,0:T(8,128)S(1)}, u32[]{:S(2)}, u32[]{:S(2)}) collective-permute-start(f32[16,512]{1,0:T(8,128)S(1)} %column_step.5.refs_4_), channel_id=1, source_target_pairs={{0,24},{4,28},{8,16},{12,20},{16,8},{20,12},{24,0},{28,4},{1,25},{... | collective-permute-start | bytes 98312 | tf_op jit(solution)/shard_map/ppermute | solution.py:36
  118.0 5.2 %row_step.5 = (f32[16,512]{1,0:T(8,128)S(1)}, f32[16,512]{1,0:T(8,128)S(1)}) custom-call(s32[66]{0:T(128)S(1)} %collect.1.refs_0_, bf16[16,64,512]{2,1,0:T(8,128)(2,1)S(1)} %get-tuple-element.18.refs_2_.refs_1_, bf16[16,64,512]{2,1,0:T(8,128)(2,1)S(1)} %get-tuple-element.19.refs_1_.refs_2_, f32[16,512]{1,0:T(8,128)S(1)} %get-tuple-element.20.refs_3_, ...), custom_call_target="tpu_custom_call" | custom-call | tf_op jit(solution)/shard_map/row_step/pallas_call | solution.py:351
  124.5 2.5 %collective-permute-start.35 = (f32[16,512]{1,0:T(8,128)S(1)}, f32[16,512]{1,0:T(8,128)S(1)}, u32[]{:S(2)}, u32[]{:S(2)}) collective-permute-start(f32[16,512]{1,0:T(8,128)S(1)} %multiply_add_fusion), channel_id=1, source_target_pairs={{0,2},{1,3},{2,0},{3,1},{4,6},{5,7},{6,4},{7,5},{8,10},{9,11},{10,... | collective-permute-start | bytes 98312 | tf_op jit(solution)/shard_map/ppermute | solution.py:36
  130.1 2.7 %collective-permute-done.36 = f32[16,512]{1,0:T(8,128)S(1)} collective-permute-done((f32[16,512]{1,0:T(8,128)S(1)}, f32[16,512]{1,0:T(8,128)S(1)}, u32[]{:S(2)}, u32[]{:S(2)}) %collective-permute-start.36) | collective-permute-done | bytes 32800 | tf_op jit(solution)/shard_map/ppermute | solution.py:36
  (84 shorter events, 30.4 us)
Async XLA Ops:
  4.3 10.0 %collective-permute-start = (f32[2,132,128]{2,1,0:T(8,128)S(1)}, f32[2,132,128]{2,1,0:T(8,128)S(1)}, u32[]{:S(2)}, u32[]{:S(2)}) collective-permute-start(f32[2,132,128]{2,1,0:T(8,128)S(1)} %get-tuple-element.14.refs_0_), channel_id=1, source_target_pairs={{0,1},{1,0},{2,3},{3,2},{4,5},{5,4},{6,7},{7,6},{8,9},{9,8},{10,11... | collective-permute-start | bytes 405512 | tf_op jit(solution)/shard_map/ppermute | solution.py:36
  7.4 13.4 %collective-permute-start.1 = (f32[2,132,128]{2,1,0:T(8,128)S(1)}, f32[2,132,128]{2,1,0:T(8,128)S(1)}, u32[]{:S(2)}, u32[]{:S(2)}) collective-permute-start(f32[2,132,128]{2,1,0:T(8,128)S(1)} %get-tuple-element.14.refs_0_), channel_id=1, source_target_pairs={{0,2},{1,3},{2,0},{3,1},{4,6},{5,7},{6,4},{7,5},{8,10},{9,11},{10,... | collective-permute-start | bytes 405512 | tf_op jit(solution)/shard_map/ppermute | solution.py:36
  10.0 10.8 %collective-permute-start.2 = (f32[2,132,128]{2,1,0:T(8,128)S(1)}, f32[2,132,128]{2,1,0:T(8,128)S(1)}, u32[]{:S(2)}, u32[]{:S(2)}) collective-permute-start(f32[2,132,128]{2,1,0:T(8,128)S(1)} %get-tuple-element.14.refs_0_), channel_id=1, source_target_pairs={{0,3},{1,2},{2,1},{3,0},{4,7},{5,6},{6,5},{7,4},{8,11},{9,10},{10,... | collective-permute-start | bytes 405512 | tf_op jit(solution)/shard_map/ppermute | solution.py:36
  10.0 13.5 %collective-permute-start.3 = (f32[2,132,128]{2,1,0:T(8,128)S(1)}, f32[2,132,128]{2,1,0:T(8,128)S(1)}, u32[]{:S(2)}, u32[]{:S(2)}) collective-permute-start(f32[2,132,128]{2,1,0:T(8,128)S(1)} %get-tuple-element.14.refs_0_), channel_id=1, source_target_pairs={{0,4},{4,0},{8,12},{12,8},{16,20},{20,16},{24,28},{28,24},{1,5},{5... | collective-permute-start | bytes 405512 | tf_op jit(solution)/shard_map/ppermute | solution.py:36
  13.9 10.1 %collective-permute-start.10 = (f32[2,132,128]{2,1,0:T(8,128)S(1)}, f32[2,132,128]{2,1,0:T(8,128)S(1)}, u32[]{:S(2)}, u32[]{:S(2)}) collective-permute-start(f32[2,132,128]{2,1,0:T(8,128)S(1)} %get-tuple-element.16), channel_id=1, source_target_pairs={{0,4},{4,0},{8,12},{12,8},{16,20},{20,16},{24,28},{28,24},{1,5},{5... | collective-permute-start | bytes 405512 | tf_op jit(solution)/shard_map/ppermute | solution.py:36
  14.3 11.3 %collective-permute-start.11 = (f32[2,132,128]{2,1,0:T(8,128)S(1)}, f32[2,132,128]{2,1,0:T(8,128)S(1)}, u32[]{:S(2)}, u32[]{:S(2)}) collective-permute-start(f32[2,132,128]{2,1,0:T(8,128)S(1)} %get-tuple-element.16), channel_id=1, source_target_pairs={{0,12},{4,8},{8,4},{12,0},{16,28},{20,24},{24,20},{28,16},{1,13},{... | collective-permute-start | bytes 405512 | tf_op jit(solution)/shard_map/ppermute | solution.py:36
  20.8 9.6 %collective-permute-start.12 = (f32[2,132,128]{2,1,0:T(8,128)S(1)}, f32[2,132,128]{2,1,0:T(8,128)S(1)}, u32[]{:S(2)}, u32[]{:S(2)}) collective-permute-start(f32[2,132,128]{2,1,0:T(8,128)S(1)} %get-tuple-element.16), channel_id=1, source_target_pairs={{0,20},{4,16},{8,28},{12,24},{16,4},{20,0},{24,12},{28,8},{1,21},{... | collective-permute-start | bytes 405512 | tf_op jit(solution)/shard_map/ppermute | solution.py:36
  20.8 10.0 %collective-permute-start.13 = (f32[2,132,128]{2,1,0:T(8,128)S(1)}, f32[2,132,128]{2,1,0:T(8,128)S(1)}, u32[]{:S(2)}, u32[]{:S(2)}) collective-permute-start(f32[2,132,128]{2,1,0:T(8,128)S(1)} %get-tuple-element.16), channel_id=1, source_target_pairs={{0,28},{4,24},{8,20},{12,16},{16,12},{20,8},{24,4},{28,0},{1,29},{... | collective-permute-start | bytes 405512 | tf_op jit(solution)/shard_map/ppermute | solution.py:36
  23.5 8.1 %collective-permute-start.7 = (f32[2,132,128]{2,1,0:T(8,128)S(1)}, f32[2,132,128]{2,1,0:T(8,128)S(1)}, u32[]{:S(2)}, u32[]{:S(2)}) collective-permute-start(f32[2,132,128]{2,1,0:T(8,128)S(1)} %get-tuple-element.15.refs_8_), channel_id=1, source_target_pairs={{0,8},{4,12},{8,0},{12,4},{16,24},{20,28},{24,16},{28,20},{1,9},{5... | collective-permute-start | bytes 405512 | tf_op jit(solution)/shard_map/ppermute | solution.py:36
  24.1 11.7 %collective-permute-start.8 = (f32[2,132,128]{2,1,0:T(8,128)S(1)}, f32[2,132,128]{2,1,0:T(8,128)S(1)}, u32[]{:S(2)}, u32[]{:S(2)}) collective-permute-start(f32[2,132,128]{2,1,0:T(8,128)S(1)} %get-tuple-element.15.refs_8_), channel_id=1, source_target_pairs={{0,16},{4,20},{8,24},{12,28},{16,0},{20,4},{24,8},{28,12},{1,17},{... | collective-permute-start | bytes 405512 | tf_op jit(solution)/shard_map/ppermute | solution.py:36
  25.6 10.2 %collective-permute-start.9 = (f32[2,132,128]{2,1,0:T(8,128)S(1)}, f32[2,132,128]{2,1,0:T(8,128)S(1)}, u32[]{:S(2)}, u32[]{:S(2)}) collective-permute-start(f32[2,132,128]{2,1,0:T(8,128)S(1)} %get-tuple-element.15.refs_8_), channel_id=1, source_target_pairs={{0,24},{4,28},{8,16},{12,20},{16,8},{20,12},{24,0},{28,4},{1,25},{... | collective-permute-start | bytes 405512 | tf_op jit(solution)/shard_map/ppermute | solution.py:36
  30.4 5.4 %collective-permute-start.4 = (f32[2,132,128]{2,1,0:T(8,128)S(1)}, f32[2,132,128]{2,1,0:T(8,128)S(1)}, u32[]{:S(2)}, u32[]{:S(2)}) collective-permute-start(f32[2,132,128]{2,1,0:T(8,128)S(1)} %collective-permute-done.refs_1_), channel_id=1, source_target_pairs={{0,4},{4,0},{8,12},{12,8},{16,20},{20,16},{24,28},{28,24},{1,5},{5... | collective-permute-start | bytes 405512 | tf_op jit(solution)/shard_map/ppermute | solution.py:36
  30.8 5.0 %collective-permute-start.5 = (f32[2,132,128]{2,1,0:T(8,128)S(1)}, f32[2,132,128]{2,1,0:T(8,128)S(1)}, u32[]{:S(2)}, u32[]{:S(2)}) collective-permute-start(f32[2,132,128]{2,1,0:T(8,128)S(1)} %collective-permute-done.1.refs_2_), channel_id=1, source_target_pairs={{0,4},{4,0},{8,12},{12,8},{16,20},{20,16},{24,28},{28,24},{1,5},{5... | collective-permute-start | bytes 405512 | tf_op jit(solution)/shard_map/ppermute | solution.py:36
  64.3 6.9 %collective-permute-start.20 = (f32[16,512]{1,0:T(8,128)S(1)}, f32[16,512]{1,0:T(8,128)S(1)}, u32[]{:S(2)}, u32[]{:S(2)}) collective-permute-start(f32[16,512]{1,0:T(8,128)S(1)} %multiply_add_fusion.2.refs_4_), channel_id=1, source_target_pairs={{0,1},{1,0},{2,3},{3,2},{4,5},{5,4},{6,7},{7,6},{8,9},{9,8},{10,11... | collective-permute-start | bytes 98312 | tf_op jit(solution)/shard_map/ppermute | solution.py:36
  66.9 6.8 %collective-permute-start.21 = (f32[16,512]{1,0:T(8,128)S(1)}, f32[16,512]{1,0:T(8,128)S(1)}, u32[]{:S(2)}, u32[]{:S(2)}) collective-permute-start(f32[16,512]{1,0:T(8,128)S(1)} %multiply_add_fusion.2.refs_4_), channel_id=1, source_target_pairs={{0,2},{1,3},{2,0},{3,1},{4,6},{5,7},{6,4},{7,5},{8,10},{9,11},{10,... | collective-permute-start | bytes 98312 | tf_op jit(solution)/shard_map/ppermute | solution.py:36
  71.2 5.7 %collective-permute-start.22 = (f32[16,512]{1,0:T(8,128)S(1)}, f32[16,512]{1,0:T(8,128)S(1)}, u32[]{:S(2)}, u32[]{:S(2)}) collective-permute-start(f32[16,512]{1,0:T(8,128)S(1)} %multiply_add_fusion.2.refs_4_), channel_id=1, source_target_pairs={{0,3},{1,2},{2,1},{3,0},{4,7},{5,6},{6,5},{7,4},{8,11},{9,10},{10,... | collective-permute-start | bytes 98312 | tf_op jit(solution)/shard_map/ppermute | solution.py:36
  82.1 7.8 %collective-permute-start.23 = (f32[16,512]{1,0:T(8,128)S(1)}, f32[16,512]{1,0:T(8,128)S(1)}, u32[]{:S(2)}, u32[]{:S(2)}) collective-permute-start(f32[16,512]{1,0:T(8,128)S(1)} %column_step.4.refs_4_.refs_8_), channel_id=1, source_target_pairs={{0,8},{4,12},{8,0},{12,4},{16,24},{20,28},{24,16},{28,20},{1,9},{5... | collective-permute-start | bytes 98312 | tf_op jit(solution)/shard_map/ppermute | solution.py:36
  82.1 9.6 %collective-permute-start.24 = (f32[16,512]{1,0:T(8,128)S(1)}, f32[16,512]{1,0:T(8,128)S(1)}, u32[]{:S(2)}, u32[]{:S(2)}) collective-permute-start(f32[16,512]{1,0:T(8,128)S(1)} %column_step.4.refs_4_.refs_8_), channel_id=1, source_target_pairs={{0,16},{4,20},{8,24},{12,28},{16,0},{20,4},{24,8},{28,12},{1,17},{... | collective-permute-start | bytes 98312 | tf_op jit(solution)/shard_map/ppermute | solution.py:36
  101.1 6.5 %collective-permute-start.29 = (f32[16,512]{1,0:T(8,128)S(1)}, f32[16,512]{1,0:T(8,128)S(1)}, u32[]{:S(2)}, u32[]{:S(2)}) collective-permute-start(f32[16,512]{1,0:T(8,128)S(1)} %multiply_add_fusion.1.refs_4_), channel_id=1, source_target_pairs={{0,3},{1,2},{2,1},{3,0},{4,7},{5,6},{6,5},{7,4},{8,11},{9,10},{10,... | collective-permute-start | bytes 98312 | tf_op jit(solution)/shard_map/ppermute | solution.py:36
  112.7 5.3 %collective-permute-start.32 = (f32[16,512]{1,0:T(8,128)S(1)}, f32[16,512]{1,0:T(8,128)S(1)}, u32[]{:S(2)}, u32[]{:S(2)}) collective-permute-start(f32[16,512]{1,0:T(8,128)S(1)} %column_step.5.refs_4_), channel_id=1, source_target_pairs={{0,24},{4,28},{8,16},{12,20},{16,8},{20,12},{24,0},{28,4},{1,25},{... | collective-permute-start | bytes 98312 | tf_op jit(solution)/shard_map/ppermute | solution.py:36
  123.2 5.7 %collective-permute-start.37 = (f32[16,512]{1,0:T(8,128)S(1)}, f32[16,512]{1,0:T(8,128)S(1)}, u32[]{:S(2)}, u32[]{:S(2)}) collective-permute-start(f32[16,512]{1,0:T(8,128)S(1)} %multiply_subtract_fusion), channel_id=1, source_target_pairs={{0,4},{4,0},{8,12},{12,8},{16,20},{20,16},{24,28},{28,24},{1,5},{5... | collective-permute-start | bytes 98312 | tf_op jit(solution)/shard_map/ppermute | solution.py:36
  124.5 5.3 %collective-permute-start.34 = (f32[16,512]{1,0:T(8,128)S(1)}, f32[16,512]{1,0:T(8,128)S(1)}, u32[]{:S(2)}, u32[]{:S(2)}) collective-permute-start(f32[16,512]{1,0:T(8,128)S(1)} %multiply_add_fusion), channel_id=1, source_target_pairs={{0,1},{1,0},{2,3},{3,2},{4,5},{5,4},{6,7},{7,6},{8,9},{9,8},{10,11... | collective-permute-start | bytes 98312 | tf_op jit(solution)/shard_map/ppermute | solution.py:36
  124.5 5.6 %collective-permute-start.35 = (f32[16,512]{1,0:T(8,128)S(1)}, f32[16,512]{1,0:T(8,128)S(1)}, u32[]{:S(2)}, u32[]{:S(2)}) collective-permute-start(f32[16,512]{1,0:T(8,128)S(1)} %multiply_add_fusion), channel_id=1, source_target_pairs={{0,2},{1,3},{2,0},{3,1},{4,6},{5,7},{6,4},{7,5},{8,10},{9,11},{10,... | collective-permute-start | bytes 98312 | tf_op jit(solution)/shard_map/ppermute | solution.py:36
  127.0 5.7 %collective-permute-start.36 = (f32[16,512]{1,0:T(8,128)S(1)}, f32[16,512]{1,0:T(8,128)S(1)}, u32[]{:S(2)}, u32[]{:S(2)}) collective-permute-start(f32[16,512]{1,0:T(8,128)S(1)} %multiply_add_fusion), channel_id=1, source_target_pairs={{0,3},{1,2},{2,1},{3,0},{4,7},{5,6},{6,5},{7,4},{8,11},{9,10},{10,... | collective-permute-start | bytes 98312 | tf_op jit(solution)/shard_map/ppermute | solution.py:36
  (20 other events, 58.2 us)
where the time goes:
time: 134 us; the launch traced here: 133 us
  starting transfers between devices  46.5 us (35%)
  Pallas kernels  43.8 us (33%)
  waiting for transfers between devices  36.1 us (27%)
  local copies, waits for them, and re-layouts  5.29 us (4%)
  between operations  1.53 us (1%)
    ppermute x38, starting transfers between devices, swap(): return jax.tree.map(lambda part: lax.ppermute(part, axis, pairs), value)  46.5 us
    pallas_call x6, Pallas kernels, half_step(): pl.pallas_call(kernel, out_shape=out_shape, in_specs=[SM] + [VM] * (3 + n...  41.1 us
    ppermute x38, waiting for transfers between devices, swap(): return jax.tree.map(lambda part: lax.ppermute(part, axis, pairs), value)  36.1 us
    unnamed x13, local copies, waits for them, and re-layouts  4.51 us
  transfers between devices with their start and end apart: 38, of which 23 were waited for; matrix products, arithmetic and copies ran while one was open for 1% of the time, Pallas kernels for 1%

commit v1 on v0

--- a/solution.py
+++ b/solution.py
@@ -26,7 +26,6 @@
 
 
 VM = pl.BlockSpec(memory_space=pltpu.VMEM)
-HBM = pl.BlockSpec(memory_space=pltpu.HBM)
 SM = pl.BlockSpec(memory_space=pltpu.SMEM)
 PARAMS = pltpu.CompilerParams(vmem_limit_bytes=24 * 1024 * 1024)
 
@@ -36,71 +35,76 @@
     return jax.tree.map(lambda part: lax.ppermute(part, axis, pairs), value)
 
 
-def pack_kernel(xt_ref, wx_hbm, yt_ref, wy_hbm, *refs):
-    *outs, wx_ref, wy_ref, sem = refs
-    dim = xt_ref.shape[0]
+def pack_kernel(points_ref, weights_ref, *outs):
+    dim = points_ref.shape[0]
     chunks = TILE // LANES
-    copies = [(wx_hbm, wx_ref), (wy_hbm, wy_ref)]
-    stores = []
-
-    def put(out, b, points_ref, weights_ref, block):
-        start = pl.multiple_of(block * TILE, TILE)
+
+    def put(out, b, block):
         for j in range(chunks):
-            source = points_ref.at[:, pl.ds(start + j * LANES, LANES)]
-            copies.append((source, out.at[b, pl.ds(j * dim, dim), :]))
-        stores.append((out, b, weights_ref, block))
+            start = pl.multiple_of(block * TILE + j * LANES, LANES)
+            out[b, j * dim : (j + 1) * dim, :] = points_ref[:, pl.ds(start, LANES)]
+        out[b, chunks * dim : chunks * (dim + 1), :] = weights_ref[pl.ds(block * chunks, chunks), :]
 
     x_ref, keep_ref, *send_refs = outs
-    for b in range(x_ref.shape[0]):
-        put(x_ref, b, xt_ref, wx_ref, b)
+    first = x_ref.shape[0]
+    for b in range(first):
+        put(x_ref, b, b)
     if send_refs:
         parity = lax.rem(lax.axis_index("row"), 2)
         for b in range(keep_ref.shape[0]):
-            put(send_refs[0], b, yt_ref, wy_ref, 2 * b + 1 - parity)
-        for b in range(keep_ref.shape[0]):
-            put(keep_ref, b, yt_ref, wy_ref, 2 * b + parity)
+            put(send_refs[0], b, first + 2 * b + 1 - parity)
+            put(keep_ref, b, first + 2 * b + parity)
     else:
         for b in range(keep_ref.shape[0]):
-            put(keep_ref, b, yt_ref, wy_ref, b)
-    started = [pltpu.make_async_copy(a, b, sem.at[i]) for i, (a, b) in enumerate(copies)]
-    for copy in started:
-        copy.start()
-    for copy in started[:2]:
-        copy.wait()
-    for out, b, weights_ref, block in stores:
-        out[b, chunks * dim : chunks * (dim + 1), :] = weights_ref[pl.ds(block * chunks, chunks), :]
-    for copy in started[2:]:
-        copy.wait()
+            put(keep_ref, b, first + b)
 
 
 def collect_tiles(tiles_own, tiles_partner, row_blocks, col_blocks):
     slots = tiles_own.shape[0] - 1
 
-    def kernel(t_own, t_partner, found):
+    firsts = (2 * slots + 2, 2 * slots + 2 + 2 * row_blocks + 2)
+
+    def kernel(t_own, t_partner, found, seen_row, seen_col):
         parity = lax.rem(lax.axis_index("row"), 2)
+        for seen in (seen_row, seen_col):
+            for i in range(seen.shape[0]):
+                seen[i] = 0
 
         def collect(ref, side, filled):
             def visit(k, filled):
+                n, rows, cols = filled
                 tile = ref[k]
-                r, c = lax.div(tile, col_blocks), lax.rem(tile, col_blocks)
-                found[filled] = (side * row_blocks + r) * CODE + lax.div(c, 2)
-                return filled + (lax.rem(c, 2) == parity).astype(jnp.int32)
+                r, c = side * row_blocks + lax.div(tile, col_blocks), lax.rem(tile, col_blocks)
+                mine = (lax.rem(c, 2) == parity).astype(jnp.int32)
+                c = lax.div(c, 2)
+                code = r * CODE + c
+                found[n] = code
+                new_row, new_col = mine * (1 - seen_row[r]), mine * (1 - seen_col[c])
+                found[rows] = code
+                found[cols] = code
+                seen_row[r] = seen_row[r] | mine
+                seen_col[c] = seen_col[c] | mine
+                return (n + mine, rows + new_row, cols + new_col)
 
             return lax.fori_loop(0, ref[slots], visit, filled)
 
-        filled = collect(t_own, parity, jnp.int32(1))
+        filled = (jnp.int32(1), jnp.int32(firsts[0] + 1), jnp.int32(firsts[1] + 1))
+        filled = collect(t_own, parity, filled)
         filled = collect(t_partner, 1 - parity, filled)
-        found[0] = filled - 1
-        found[filled] = 0
-
-    return pl.pallas_call(
+        for at, end in zip((0,) + firsts, filled):
+            found[at] = end - at - 1
+            found[end] = 0
+
+    tiles = pl.pallas_call(
         kernel,
-        out_shape=jax.ShapeDtypeStruct((2 * slots + 2,), jnp.int32),
+        out_shape=jax.ShapeDtypeStruct((firsts[1] + col_blocks // 2 + 2,), jnp.int32),
         in_specs=[SM] * 2,
         out_specs=SM,
+        scratch_shapes=[pltpu.SMEM((2 * row_blocks,), jnp.int32), pltpu.SMEM((col_blocks // 2,), jnp.int32)],
         compiler_params=PARAMS,
         name="collect",
     )(tiles_own, tiles_partner)
+    return tiles, firsts
 
 
 def prepare(own_x, partner_x, own_y, partner_y, dual_own, dual_partner, sizes):
@@ -198,7 +202,7 @@
     return peak + jnp.log2(total)
 
 
-def half_step(from_points, to_points, weights, parts, guess, tiles, from_first, keep_total):
+def half_step(from_points, to_points, weights, parts, guess, tiles, first, from_first, keep_total):
     m_blocks, width, _ = from_points.shape
     n_blocks = to_points.shape[0]
     dim = width // 2
@@ -207,19 +211,20 @@
     guessed = guess is not None
 
     def kernel(*refs):
-        tiles_ref, a_ref, b_ref, w_ref = refs[:4]
+        listed_ref, a_ref, b_ref, w_ref = refs[:4]
         part_refs = refs[4 : 4 + n_parts]
         rest = list(refs[4 + n_parts :])
         guess_ref = rest.pop(0) if guessed else None
         out_ref = rest.pop(0)
         total_ref = rest.pop(0) if keep_total else None
-        lifts, drops, peaks, sums, s0, s1, p0, p1 = rest
-        n = tiles_ref[0]
-
-        def ends(k):
-            code = tiles_ref[jnp.minimum(k, n) + 1]
-            first, second = lax.shift_right_logical(code, SHIFT), code & (CODE - 1)
-            return (first, second) if from_first else (second, first)
+        lifts, drops, peaks, sums, s0, s1, p0, p1, tiles_ref, arrived = rest
+        listing = pltpu.make_async_copy(listed_ref, tiles_ref, arrived)
+        listing.start()
+
+        def ends(k, base=0):
+            code = tiles_ref[base + jnp.minimum(k, tiles_ref[base]) + 1]
+            above, below = lax.shift_right_logical(code, SHIFT), code & (CODE - 1)
+            return (above, below) if from_first else (below, above)
 
 
         if n_parts:
@@ -245,6 +250,14 @@
 
         pieces(lifts, lift, 0, 3)
         plain = jnp.where(place < 3, 1.0, 0.0).astype(jnp.bfloat16)
+        if guessed:
+            shift = guess_ref[...]
+            used = shift > 0.5 * lowest
+            shift = jnp.where(used, shift, 0.0)
+            pieces(drops, -shift, 3, 0)
+        sums[...] = jnp.zeros(sums.shape, jnp.float32)
+        listing.wait()
+        n = tiles_ref[0]
 
         def doubled(ref, i, high_first):
             both = ref[i]
@@ -252,15 +265,15 @@
                 return [both[0:dim], both]
             return [both, both[0:dim]]
 
-        def product(k, shifted, rows=TILE):
-            m, c = ends(k)
+        def product(k, shifted, rows=TILE, base=0):
+            m, c = ends(k, base)
             left = jnp.concatenate(doubled(a_ref, m, not from_first) + [lifts[m]], axis=0)[:, :rows]
             right = jnp.concatenate(doubled(b_ref, c, from_first) + [drops[c] if shifted else plain], axis=0)
             value = lax.dot_general(left, right, (((0,), (0,)), ((), ())), preferred_element_type=jnp.float32)
             return value.reshape(rows // 8, 8, TILE)
 
-        def target(k):
-            return jnp.where(k < n, ends(k)[1], n_blocks)
+        def target(k, base=0):
+            return jnp.where(k < tiles_ref[base], ends(k, base)[1], n_blocks)
 
         def exact():
             peaks[...] = jnp.full(peaks.shape, lowest, jnp.float32)
@@ -294,27 +307,23 @@
             total = jnp.sum(sums[0:n_blocks] * jnp.exp2(top - peak[:, None, :]), axis=1)
             out_ref[...] = jnp.where(total > 0.0, peak + jnp.log2(total), lowest)
 
-        batches = lax.div(n + UNROLL - 1, UNROLL)
-        if guessed:
-            shift = guess_ref[...]
-        else:
+        if not guessed:
             peaks[...] = jnp.full(peaks.shape, lowest, jnp.float32)
 
             def look(step, carry):
                 found = []
                 for u in range(UNROLL):
                     k = UNROLL * step + u
-                    found.append((target(k), jnp.max(product(k, False, SAMPLE), axis=0)))
+                    found.append((target(k, first), jnp.max(product(k, False, SAMPLE, first), axis=0)))
                 for c, peak in found:
                     peaks[c] = jnp.maximum(peaks[c], peak)
                 return carry
 
-            lax.fori_loop(0, batches, look, 0)
+            lax.fori_loop(0, lax.div(tiles_ref[first] + UNROLL - 1, UNROLL), look, 0)
             shift = jnp.max(peaks[0:n_blocks], axis=1) + MARGIN
-        used = shift > 0.5 * lowest
-        shift = jnp.where(used, shift, 0.0)
-        pieces(drops, -shift, 3, 0)
-        sums[...] = jnp.zeros(sums.shape, jnp.float32)
+            used = shift > 0.5 * lowest
+            shift = jnp.where(used, shift, 0.0)
+            pieces(drops, -shift, 3, 0)
 
         def batch(start, size):
             found = []
@@ -351,7 +360,7 @@
     return pl.pallas_call(
         kernel,
         out_shape=out_shape,
-        in_specs=[SM] + [VM] * (3 + n_parts + len(extra)),
+        in_specs=[VM] * (4 + n_parts + len(extra)),
         out_specs=[VM] * len(out_shape),
         scratch_shapes=[
             pltpu.VMEM((m_blocks, BIAS, TILE), jnp.bfloat16),
@@ -362,6 +371,8 @@
             pltpu.VMEM((groups, 8, TILE), f32),
             pltpu.VMEM((8, TILE), f32),
             pltpu.VMEM((8, TILE), f32),
+            pltpu.SMEM(tiles.shape, jnp.int32),
+            pltpu.SemaphoreType.DMA(()),
         ],
         compiler_params=PARAMS,
         name="column_step" if from_first else "row_step",
@@ -387,20 +398,13 @@
     packed = pl.pallas_call(
         pack_kernel,
         out_shape=packed_shapes,
-        in_specs=[HBM] * 4,
+        in_specs=[VM] * 2,
         out_specs=[VM] * len(packed_shapes),
-        scratch_shapes=[
-            pltpu.VMEM((own_row_blocks * chunks, LANES), jnp.float32),
-            pltpu.VMEM((own_col_blocks * chunks, LANES), jnp.float32),
-            pltpu.SemaphoreType.DMA((chunks * (own_row_blocks + own_col_blocks) + 2,)),
-        ],
         compiler_params=PARAMS,
         name="pack",
     )(
-        samples.T,
-        sample_logw.reshape(-1, LANES),
-        references.T,
-        reference_logw.reshape(-1, LANES),
+        jnp.concatenate([samples.T, references.T], axis=1),
+        jnp.concatenate([sample_logw, reference_logw]).reshape(-1, LANES),
     )
     x_pack, y_keep = packed[0], packed[1]
     sends = [("col", d, x_pack) for d in range(n_col - 1, 0, -1)]
@@ -413,7 +417,7 @@
         order += sends[:1] + plane[:pace]
         sends, plane = sends[1:], plane[pace:]
     tiles_own = jnp.concatenate([kept_tiles[0, 0], tile_counts[0]])
-    order[2:2] = [("row", 0, tiles_own), ("row", -1, dual_start)]
+    order[7:7] = [("row", 0, tiles_own), ("row", -1, dual_start)]
     got = {}
     for axis, distance, value in order:
         got[axis, distance] = swap(value, axis, distance if distance > 0 else 1)
@@ -422,7 +426,7 @@
     own_x = [x_pack] + [got["col", d] for d in range(1, n_col)]
     partner_x = [swap(part, "row", 1) for part in own_x]
     tiles_partner, dual_partner = got["row", 0], got["row", -1]
-    tiles = collect_tiles(tiles_own, tiles_partner, row_blocks, col_blocks)
+    tiles, firsts = collect_tiles(tiles_own, tiles_partner, row_blocks, col_blocks)
     xp, yp, start, wx, wy, nx, ny = prepare(
         own_x, partner_x, own_y, partner_y, dual_start, dual_partner, (row_blocks, col_blocks, dim)
     )
@@ -431,23 +435,42 @@
     col_guess = row_guess = None
     for turn in range(ITERS):
         last = turn == ITERS - 1
-        (part,) = half_step(xp, yp, wx if turn else start, row_parts, col_guess, tiles, True, False)
+        (part,) = half_step(xp, yp, wx if turn else start, row_parts, col_guess, tiles, firsts[1], True, False)
         col_guess = part
         col_parts = [part] + [swap(part, "row", 2 * d) for d in range(1, n_row // 2)]
-        part, *kept_total = half_step(yp, xp, wy, col_parts, row_guess, tiles, False, last)
+        part, *kept_total = half_step(yp, xp, wy, col_parts, row_guess, tiles, firsts[0], False, last)
         row_guess = part
-        part = log_sum([part, swap(part, "row", 1)])
+        if last:
+            mine, other = (
+                lax.dynamic_slice_in_dim(part, side * row_blocks, row_blocks, 0) for side in (parity, 1 - parity)
+            )
+        else:
+            mine = other = part
+        part = log_sum([mine, swap(other, "row", 1)])
         row_parts = [part] + [swap(part, "col", d) for d in range(1, n_col)]
 
-    own = [lax.dynamic_slice_in_dim(part, parity * row_blocks, row_blocks, 0) for part in row_parts]
     norms = lax.dynamic_slice_in_dim(nx, parity * row_blocks, row_blocks, 0)
-    row_duals = norms - (epsilon * ln2) * log_sum(own)
+
+    def finish(norms_ref, *refs):
+        *parts, out = refs
+        duals = norms_ref[...] - (epsilon * ln2) * log_sum([part[...] for part in parts])
+        for b in range(row_blocks):
+            out[0:1, b * TILE : (b + 1) * TILE] = duals[b : b + 1, :]
+
+    row_duals = pl.pallas_call(
+        finish,
+        out_shape=shape(dual_start.shape, jnp.float32),
+        in_specs=[VM] * (1 + n_col),
+        out_specs=VM,
+        compiler_params=PARAMS,
+        name="finish",
+    )(norms, *row_parts)
     col_half = ny - (epsilon * ln2) * kept_total[0]
     col_other = swap(col_half, "row", 1)
     even = jnp.where(parity == 0, col_half, col_other)
     odd = jnp.where(parity == 0, col_other, col_half)
     col_duals = jnp.stack([even, odd], axis=1)
-    return (row_duals.reshape(1, -1), col_duals.reshape(1, -1))
+    return (row_duals, col_duals.reshape(1, -1))
 
 
 def solution(mesh):

time: 134 us -> 129 us (0.963)
  local copies, waits for them, and re-layouts: 5.29 us -> 1.46 us
    unnamed x13 -> x8, local copies, waits for them, and re-layouts: 4.51 us -> 0.67 us
    pallas_call x8 -> x9, Pallas kernels: 43.1 us -> 41.9 us  [the longest x6 39.5 us: half_step(): pl.pallas_call(kernel, out_shape=out_shape, in_specs=[VM] * (4 + n_parts...]
  transfers between devices with their start and end apart: 38 -> 38, of which waited for: 23 -> 22; matrix products, arithmetic and copies ran while one was open for 1% -> 1% of each run, Pallas kernels for 1% -> 1%
where the time goes in v1:
time: 129 us
  starting transfers between devices  46.3 us (36%)
  Pallas kernels  42.7 us (33%)
  waiting for transfers between devices  35.7 us (28%)
  between operations  1.57 us (1%)
  local copies, waits for them, and re-layouts  1.46 us (1%)
    ppermute x38, starting transfers between devices, swap(): return jax.tree.map(lambda part: lax.ppermute(part, axis, pairs), value)  46.3 us
    pallas_call x6, Pallas kernels, half_step(): pl.pallas_call(kernel, out_shape=out_shape, in_specs=[VM] * (4 + n_parts...  39.5 us
    ppermute x38, waiting for transfers between devices, swap(): return jax.tree.map(lambda part: lax.ppermute(part, axis, pairs), value)  35.7 us
  transfers between devices with their start and end apart: 38, of which 22 were waited for; matrix products, arithmetic and copies ran while one was open for 1% of the time, Pallas kernels for 1%

profile of v1, /device:TPU:0, one launch (start us, length us, event | category | flops | bytes accessed | tf_op | source)
XLA Modules:
  0.0 128.9 jit_solution(5061081252788714886)
XLA Ops:
  1.8 3.1 %collective-permute-start = (f32[2,132,128]{2,1,0:T(8,128)S(1)}, f32[2,132,128]{2,1,0:T(8,128)S(1)}, u32[]{:S(2)}, u32[]{:S(2)}) collective-permute-start(f32[2,132,128]{2,1,0:T(8,128)S(1)} %get-tuple-element.14.refs_0_), channel_id=1, source_target_pairs={{0,1},{1,0},{2,3},{3,2},{4,5},{5,4},{6,7},{7,6},{8,9},{9,8},{10,11... | collective-permute-start | bytes 405512 | tf_op jit(solution)/shard_map/ppermute | solution.py:35
  4.9 2.6 %collective-permute-start.1 = (f32[2,132,128]{2,1,0:T(8,128)S(1)}, f32[2,132,128]{2,1,0:T(8,128)S(1)}, u32[]{:S(2)}, u32[]{:S(2)}) collective-permute-start(f32[2,132,128]{2,1,0:T(8,128)S(1)} %get-tuple-element.14.refs_0_), channel_id=1, source_target_pairs={{0,2},{1,3},{2,0},{3,1},{4,6},{5,7},{6,4},{7,5},{8,10},{9,11},{10,... | collective-permute-start | bytes 405512 | tf_op jit(solution)/shard_map/ppermute | solution.py:35
  13.2 5.1 %collective-permute-done.1.refs_2_ = f32[2,132,128]{2,1,0:T(8,128)S(1)} collective-permute-done((f32[2,132,128]{2,1,0:T(8,128)S(1)}, f32[2,132,128]{2,1,0:T(8,128)S(1)}, u32[]{:S(2)}, u32[]{:S(2)}) %collective-permute-start.1) | collective-permute-done | bytes 135200 | tf_op jit(solution)/shard_map/ppermute | solution.py:35
  18.3 2.7 %collective-permute-start.13 = (f32[2,132,128]{2,1,0:T(8,128)S(1)}, f32[2,132,128]{2,1,0:T(8,128)S(1)}, u32[]{:S(2)}, u32[]{:S(2)}) collective-permute-start(f32[2,132,128]{2,1,0:T(8,128)S(1)} %get-tuple-element.16), channel_id=1, source_target_pairs={{0,28},{4,24},{8,20},{12,16},{16,12},{20,8},{24,4},{28,0},{1,29},{... | collective-permute-start | bytes 405512 | tf_op jit(solution)/shard_map/ppermute | solution.py:35
  24.5 3.4 %collective-permute-done.12.refs_14_ = f32[2,132,128]{2,1,0:T(8,128)S(1)} collective-permute-done((f32[2,132,128]{2,1,0:T(8,128)S(1)}, f32[2,132,128]{2,1,0:T(8,128)S(1)}, u32[]{:S(2)}, u32[]{:S(2)}) %collective-permute-start.12) | collective-permute-done | bytes 135200 | tf_op jit(solution)/shard_map/ppermute | solution.py:35
  30.9 2.4 %collective-permute-done.8.refs_10_ = f32[2,132,128]{2,1,0:T(8,128)S(1)} collective-permute-done((f32[2,132,128]{2,1,0:T(8,128)S(1)}, f32[2,132,128]{2,1,0:T(8,128)S(1)}, u32[]{:S(2)}, u32[]{:S(2)}) %collective-permute-start.8) | collective-permute-done | bytes 135200 | tf_op jit(solution)/shard_map/ppermute | solution.py:35
  34.0 5.9 %column_step.3.refs_4_.refs_8_ = f32[16,512]{1,0:T(8,128)S(1)} custom-call(s32[102]{0:T(128)S(1)} %collect.1.refs_0_, bf16[16,64,512]{2,1,0:T(8,128)(2,1)S(1)} %get-tuple-element.19.refs_1_.refs_2_, bf16[16,64,512]{2,1,0:T(8,128)(2,1)S(1)} %get-tuple-element.18.refs_2_.refs_1_, f32[16,512]{1,0:T(8,128)S(1)} %get-tuple-element.22.refs_3_), custom_call_target="tpu_custom_call" | custom-call | tf_op jit(solution)/shard_map/column_step/pallas_call | solution.py:360
  40.6 3.0 %collective-permute-start.18 = (f32[16,512]{1,0:T(8,128)S(1)}, f32[16,512]{1,0:T(8,128)S(1)}, u32[]{:S(2)}, u32[]{:S(2)}) collective-permute-start(f32[16,512]{1,0:T(8,128)S(1)} %column_step.3.refs_4_.refs_8_), channel_id=1, source_target_pairs={{0,24},{4,28},{8,16},{12,20},{16,8},{20,12},{24,0},{28,4},{1,25},{... | collective-permute-start | bytes 98312 | tf_op jit(solution)/shard_map/ppermute | solution.py:35
  45.4 14.0 %row_step.3.refs_8_ = f32[16,512]{1,0:T(8,128)S(1)} custom-call(s32[102]{0:T(128)S(1)} %collect.1.refs_0_, bf16[16,64,512]{2,1,0:T(8,128)(2,1)S(1)} %get-tuple-element.18.refs_2_.refs_1_, bf16[16,64,512]{2,1,0:T(8,128)(2,1)S(1)} %get-tuple-element.19.refs_1_.refs_2_, f32[16,512]{1,0:T(8,128)S(1)} %get-tuple-element.20.refs_3_, ...), custom_call_target="tpu_custom_call" | custom-call | tf_op jit(solution)/shard_map/row_step/pallas_call | solution.py:360
  60.8 3.2 %collective-permute-start.20 = (f32[16,512]{1,0:T(8,128)S(1)}, f32[16,512]{1,0:T(8,128)S(1)}, u32[]{:S(2)}, u32[]{:S(2)}) collective-permute-start(f32[16,512]{1,0:T(8,128)S(1)} %multiply_add_fusion.1.refs_4_), channel_id=1, source_target_pairs={{0,1},{1,0},{2,3},{3,2},{4,5},{5,4},{6,7},{7,6},{8,9},{9,8},{10,11... | collective-permute-start | bytes 98312 | tf_op jit(solution)/shard_map/ppermute | solution.py:35
  64.0 3.8 %collective-permute-start.21 = (f32[16,512]{1,0:T(8,128)S(1)}, f32[16,512]{1,0:T(8,128)S(1)}, u32[]{:S(2)}, u32[]{:S(2)}) collective-permute-start(f32[16,512]{1,0:T(8,128)S(1)} %multiply_add_fusion.1.refs_4_), channel_id=1, source_target_pairs={{0,2},{1,3},{2,0},{3,1},{4,6},{5,7},{6,4},{7,5},{8,10},{9,11},{10,... | collective-permute-start | bytes 98312 | tf_op jit(solution)/shard_map/ppermute | solution.py:35
  67.8 2.5 %collective-permute-done.21.refs_6_ = f32[16,512]{1,0:T(8,128)S(1)} collective-permute-done((f32[16,512]{1,0:T(8,128)S(1)}, f32[16,512]{1,0:T(8,128)S(1)}, u32[]{:S(2)}, u32[]{:S(2)}) %collective-permute-start.21) | collective-permute-done | bytes 32800 | tf_op jit(solution)/shard_map/ppermute | solution.py:35
  70.2 3.2 %collective-permute-done.22.refs_7_ = f32[16,512]{1,0:T(8,128)S(1)} collective-permute-done((f32[16,512]{1,0:T(8,128)S(1)}, f32[16,512]{1,0:T(8,128)S(1)}, u32[]{:S(2)}, u32[]{:S(2)}) %collective-permute-start.22) | collective-permute-done | bytes 32800 | tf_op jit(solution)/shard_map/ppermute | solution.py:35
  73.5 5.0 %column_step.4.refs_4_.refs_8_ = f32[16,512]{1,0:T(8,128)S(1)} custom-call(s32[102]{0:T(128)S(1)} %collect.1.refs_0_, bf16[16,64,512]{2,1,0:T(8,128)(2,1)S(1)} %get-tuple-element.19.refs_1_.refs_2_, bf16[16,64,512]{2,1,0:T(8,128)(2,1)S(1)} %get-tuple-element.18.refs_2_.refs_1_, f32[16,512]{1,0:T(8,128)S(1)} %get-tuple-element.21.refs_3_, ...), custom_call_target="tpu_custom_call" | custom-call | tf_op jit(solution)/shard_map/column_step/pallas_call | solution.py:360
  78.5 7.5 %collective-permute-start.24 = (f32[16,512]{1,0:T(8,128)S(1)}, f32[16,512]{1,0:T(8,128)S(1)}, u32[]{:S(2)}, u32[]{:S(2)}) collective-permute-start(f32[16,512]{1,0:T(8,128)S(1)} %column_step.4.refs_4_.refs_8_), channel_id=1, source_target_pairs={{0,16},{4,20},{8,24},{12,28},{16,0},{20,4},{24,8},{28,12},{1,17},{... | collective-permute-start | bytes 98312 | tf_op jit(solution)/shard_map/ppermute | solution.py:35
  86.0 1.9 %collective-permute-done.24.refs_6_ = f32[16,512]{1,0:T(8,128)S(1)} collective-permute-done((f32[16,512]{1,0:T(8,128)S(1)}, f32[16,512]{1,0:T(8,128)S(1)}, u32[]{:S(2)}, u32[]{:S(2)}) %collective-permute-start.24) | collective-permute-done | bytes 32800 | tf_op jit(solution)/shard_map/ppermute | solution.py:35
  87.9 2.9 %collective-permute-done.25.refs_7_ = f32[16,512]{1,0:T(8,128)S(1)} collective-permute-done((f32[16,512]{1,0:T(8,128)S(1)}, f32[16,512]{1,0:T(8,128)S(1)}, u32[]{:S(2)}, u32[]{:S(2)}) %collective-permute-start.25) | collective-permute-done | bytes 32800 | tf_op jit(solution)/shard_map/ppermute | solution.py:35
  90.9 4.8 %row_step.4.refs_8_ = f32[16,512]{1,0:T(8,128)S(1)} custom-call(s32[102]{0:T(128)S(1)} %collect.1.refs_0_, bf16[16,64,512]{2,1,0:T(8,128)(2,1)S(1)} %get-tuple-element.18.refs_2_.refs_1_, bf16[16,64,512]{2,1,0:T(8,128)(2,1)S(1)} %get-tuple-element.19.refs_1_.refs_2_, f32[16,512]{1,0:T(8,128)S(1)} %get-tuple-element.20.refs_3_, ...), custom_call_target="tpu_custom_call" | custom-call | tf_op jit(solution)/shard_map/row_step/pallas_call | solution.py:360
  97.1 4.3 %collective-permute-start.29 = (f32[16,512]{1,0:T(8,128)S(1)}, f32[16,512]{1,0:T(8,128)S(1)}, u32[]{:S(2)}, u32[]{:S(2)}) collective-permute-start(f32[16,512]{1,0:T(8,128)S(1)} %multiply_add_fusion.refs_4_), channel_id=1, source_target_pairs={{0,3},{1,2},{2,1},{3,0},{4,7},{5,6},{6,5},{7,4},{8,11},{9,10},{10,... | collective-permute-start | bytes 98312 | tf_op jit(solution)/shard_map/ppermute | solution.py:35
  103.6 5.0 %column_step.5.refs_4_ = f32[16,512]{1,0:T(8,128)S(1)} custom-call(s32[102]{0:T(128)S(1)} %collect.1.refs_0_, bf16[16,64,512]{2,1,0:T(8,128)(2,1)S(1)} %get-tuple-element.19.refs_1_.refs_2_, bf16[16,64,512]{2,1,0:T(8,128)(2,1)S(1)} %get-tuple-element.18.refs_2_.refs_1_, f32[16,512]{1,0:T(8,128)S(1)} %get-tuple-element.21.refs_3_, ...), custom_call_target="tpu_custom_call" | custom-call | tf_op jit(solution)/shard_map/column_step/pallas_call | solution.py:360
  108.8 3.4 %collective-permute-start.32 = (f32[16,512]{1,0:T(8,128)S(1)}, f32[16,512]{1,0:T(8,128)S(1)}, u32[]{:S(2)}, u32[]{:S(2)}) collective-permute-start(f32[16,512]{1,0:T(8,128)S(1)} %column_step.5.refs_4_), channel_id=1, source_target_pairs={{0,24},{4,28},{8,16},{12,20},{16,8},{20,12},{24,0},{28,4},{1,25},{... | collective-permute-start | bytes 98312 | tf_op jit(solution)/shard_map/ppermute | solution.py:35
  114.1 4.8 %row_step.5 = (f32[16,512]{1,0:T(8,128)S(1)}, f32[16,512]{1,0:T(8,128)S(1)}) custom-call(s32[102]{0:T(128)S(1)} %collect.1.refs_0_, bf16[16,64,512]{2,1,0:T(8,128)(2,1)S(1)} %get-tuple-element.18.refs_2_.refs_1_, bf16[16,64,512]{2,1,0:T(8,128)(2,1)S(1)} %get-tuple-element.19.refs_1_.refs_2_, f32[16,512]{1,0:T(8,128)S(1)} %get-tuple-element.20.refs_3_, ...), custom_call_target="tpu_custom_call" | custom-call | tf_op jit(solution)/shard_map/row_step/pallas_call | solution.py:360
  120.3 2.5 %collective-permute-start.35 = (f32[8,512]{1,0:T(8,128)S(1)}, f32[8,512]{1,0:T(8,128)S(1)}, u32[]{:S(2)}, u32[]{:S(2)}) collective-permute-start(f32[8,512]{1,0:T(8,128)S(1)} %multiply_add_fusion.2.refs_0_), channel_id=1, source_target_pairs={{0,2},{1,3},{2,0},{3,1},{4,6},{5,7},{6,4},{7,5},{8,10},{9,11},{10,... | collective-permute-start | bytes 49160 | tf_op jit(solution)/shard_map/ppermute | solution.py:35
  125.5 2.8 %collective-permute-done.36.refs_3_ = f32[8,512]{1,0:T(8,128)S(1)} collective-permute-done((f32[8,512]{1,0:T(8,128)S(1)}, f32[8,512]{1,0:T(8,128)S(1)}, u32[]{:S(2)}, u32[]{:S(2)}) %collective-permute-start.36) | collective-permute-done | bytes 16416 | tf_op jit(solution)/shard_map/ppermute | solution.py:35
  (83 shorter events, 27.6 us)
Async XLA Ops:
  1.8 10.0 %collective-permute-start = (f32[2,132,128]{2,1,0:T(8,128)S(1)}, f32[2,132,128]{2,1,0:T(8,128)S(1)}, u32[]{:S(2)}, u32[]{:S(2)}) collective-permute-start(f32[2,132,128]{2,1,0:T(8,128)S(1)} %get-tuple-element.14.refs_0_), channel_id=1, source_target_pairs={{0,1},{1,0},{2,3},{3,2},{4,5},{5,4},{6,7},{7,6},{8,9},{9,8},{10,11... | collective-permute-start | bytes 405512 | tf_op jit(solution)/shard_map/ppermute | solution.py:35
  4.9 13.4 %collective-permute-start.1 = (f32[2,132,128]{2,1,0:T(8,128)S(1)}, f32[2,132,128]{2,1,0:T(8,128)S(1)}, u32[]{:S(2)}, u32[]{:S(2)}) collective-permute-start(f32[2,132,128]{2,1,0:T(8,128)S(1)} %get-tuple-element.14.refs_0_), channel_id=1, source_target_pairs={{0,2},{1,3},{2,0},{3,1},{4,6},{5,7},{6,4},{7,5},{8,10},{9,11},{10,... | collective-permute-start | bytes 405512 | tf_op jit(solution)/shard_map/ppermute | solution.py:35
  7.5 10.8 %collective-permute-start.2 = (f32[2,132,128]{2,1,0:T(8,128)S(1)}, f32[2,132,128]{2,1,0:T(8,128)S(1)}, u32[]{:S(2)}, u32[]{:S(2)}) collective-permute-start(f32[2,132,128]{2,1,0:T(8,128)S(1)} %get-tuple-element.14.refs_0_), channel_id=1, source_target_pairs={{0,3},{1,2},{2,1},{3,0},{4,7},{5,6},{6,5},{7,4},{8,11},{9,10},{10,... | collective-permute-start | bytes 405512 | tf_op jit(solution)/shard_map/ppermute | solution.py:35
  7.5 13.5 %collective-permute-start.3 = (f32[2,132,128]{2,1,0:T(8,128)S(1)}, f32[2,132,128]{2,1,0:T(8,128)S(1)}, u32[]{:S(2)}, u32[]{:S(2)}) collective-permute-start(f32[2,132,128]{2,1,0:T(8,128)S(1)} %get-tuple-element.14.refs_0_), channel_id=1, source_target_pairs={{0,4},{4,0},{8,12},{12,8},{16,20},{20,16},{24,28},{28,24},{1,5},{5... | collective-permute-start | bytes 405512 | tf_op jit(solution)/shard_map/ppermute | solution.py:35
  11.4 10.1 %collective-permute-start.10 = (f32[2,132,128]{2,1,0:T(8,128)S(1)}, f32[2,132,128]{2,1,0:T(8,128)S(1)}, u32[]{:S(2)}, u32[]{:S(2)}) collective-permute-start(f32[2,132,128]{2,1,0:T(8,128)S(1)} %get-tuple-element.16), channel_id=1, source_target_pairs={{0,4},{4,0},{8,12},{12,8},{16,20},{20,16},{24,28},{28,24},{1,5},{5... | collective-permute-start | bytes 405512 | tf_op jit(solution)/shard_map/ppermute | solution.py:35
  11.7 11.3 %collective-permute-start.11 = (f32[2,132,128]{2,1,0:T(8,128)S(1)}, f32[2,132,128]{2,1,0:T(8,128)S(1)}, u32[]{:S(2)}, u32[]{:S(2)}) collective-permute-start(f32[2,132,128]{2,1,0:T(8,128)S(1)} %get-tuple-element.16), channel_id=1, source_target_pairs={{0,12},{4,8},{8,4},{12,0},{16,28},{20,24},{24,20},{28,16},{1,13},{... | collective-permute-start | bytes 405512 | tf_op jit(solution)/shard_map/ppermute | solution.py:35
  18.3 9.6 %collective-permute-start.12 = (f32[2,132,128]{2,1,0:T(8,128)S(1)}, f32[2,132,128]{2,1,0:T(8,128)S(1)}, u32[]{:S(2)}, u32[]{:S(2)}) collective-permute-start(f32[2,132,128]{2,1,0:T(8,128)S(1)} %get-tuple-element.16), channel_id=1, source_target_pairs={{0,20},{4,16},{8,28},{12,24},{16,4},{20,0},{24,12},{28,8},{1,21},{... | collective-permute-start | bytes 405512 | tf_op jit(solution)/shard_map/ppermute | solution.py:35
  18.3 10.0 %collective-permute-start.13 = (f32[2,132,128]{2,1,0:T(8,128)S(1)}, f32[2,132,128]{2,1,0:T(8,128)S(1)}, u32[]{:S(2)}, u32[]{:S(2)}) collective-permute-start(f32[2,132,128]{2,1,0:T(8,128)S(1)} %get-tuple-element.16), channel_id=1, source_target_pairs={{0,28},{4,24},{8,20},{12,16},{16,12},{20,8},{24,4},{28,0},{1,29},{... | collective-permute-start | bytes 405512 | tf_op jit(solution)/shard_map/ppermute | solution.py:35
  21.0 8.1 %collective-permute-start.7 = (f32[2,132,128]{2,1,0:T(8,128)S(1)}, f32[2,132,128]{2,1,0:T(8,128)S(1)}, u32[]{:S(2)}, u32[]{:S(2)}) collective-permute-start(f32[2,132,128]{2,1,0:T(8,128)S(1)} %get-tuple-element.15.refs_8_), channel_id=1, source_target_pairs={{0,8},{4,12},{8,0},{12,4},{16,24},{20,28},{24,16},{28,20},{1,9},{5... | collective-permute-start | bytes 405512 | tf_op jit(solution)/shard_map/ppermute | solution.py:35
  21.5 11.7 %collective-permute-start.8 = (f32[2,132,128]{2,1,0:T(8,128)S(1)}, f32[2,132,128]{2,1,0:T(8,128)S(1)}, u32[]{:S(2)}, u32[]{:S(2)}) collective-permute-start(f32[2,132,128]{2,1,0:T(8,128)S(1)} %get-tuple-element.15.refs_8_), channel_id=1, source_target_pairs={{0,16},{4,20},{8,24},{12,28},{16,0},{20,4},{24,8},{28,12},{1,17},{... | collective-permute-start | bytes 405512 | tf_op jit(solution)/shard_map/ppermute | solution.py:35
  23.1 10.2 %collective-permute-start.9 = (f32[2,132,128]{2,1,0:T(8,128)S(1)}, f32[2,132,128]{2,1,0:T(8,128)S(1)}, u32[]{:S(2)}, u32[]{:S(2)}) collective-permute-start(f32[2,132,128]{2,1,0:T(8,128)S(1)} %get-tuple-element.15.refs_8_), channel_id=1, source_target_pairs={{0,24},{4,28},{8,16},{12,20},{16,8},{20,12},{24,0},{28,4},{1,25},{... | collective-permute-start | bytes 405512 | tf_op jit(solution)/shard_map/ppermute | solution.py:35
  27.9 5.4 %collective-permute-start.4 = (f32[2,132,128]{2,1,0:T(8,128)S(1)}, f32[2,132,128]{2,1,0:T(8,128)S(1)}, u32[]{:S(2)}, u32[]{:S(2)}) collective-permute-start(f32[2,132,128]{2,1,0:T(8,128)S(1)} %collective-permute-done.refs_1_), channel_id=1, source_target_pairs={{0,4},{4,0},{8,12},{12,8},{16,20},{20,16},{24,28},{28,24},{1,5},{5... | collective-permute-start | bytes 405512 | tf_op jit(solution)/shard_map/ppermute | solution.py:35
  28.3 5.0 %collective-permute-start.5 = (f32[2,132,128]{2,1,0:T(8,128)S(1)}, f32[2,132,128]{2,1,0:T(8,128)S(1)}, u32[]{:S(2)}, u32[]{:S(2)}) collective-permute-start(f32[2,132,128]{2,1,0:T(8,128)S(1)} %collective-permute-done.1.refs_2_), channel_id=1, source_target_pairs={{0,4},{4,0},{8,12},{12,8},{16,20},{20,16},{24,28},{28,24},{1,5},{5... | collective-permute-start | bytes 405512 | tf_op jit(solution)/shard_map/ppermute | solution.py:35
  60.8 7.0 %collective-permute-start.20 = (f32[16,512]{1,0:T(8,128)S(1)}, f32[16,512]{1,0:T(8,128)S(1)}, u32[]{:S(2)}, u32[]{:S(2)}) collective-permute-start(f32[16,512]{1,0:T(8,128)S(1)} %multiply_add_fusion.1.refs_4_), channel_id=1, source_target_pairs={{0,1},{1,0},{2,3},{3,2},{4,5},{5,4},{6,7},{7,6},{8,9},{9,8},{10,11... | collective-permute-start | bytes 98312 | tf_op jit(solution)/shard_map/ppermute | solution.py:35
  64.0 6.2 %collective-permute-start.21 = (f32[16,512]{1,0:T(8,128)S(1)}, f32[16,512]{1,0:T(8,128)S(1)}, u32[]{:S(2)}, u32[]{:S(2)}) collective-permute-start(f32[16,512]{1,0:T(8,128)S(1)} %multiply_add_fusion.1.refs_4_), channel_id=1, source_target_pairs={{0,2},{1,3},{2,0},{3,1},{4,6},{5,7},{6,4},{7,5},{8,10},{9,11},{10,... | collective-permute-start | bytes 98312 | tf_op jit(solution)/shard_map/ppermute | solution.py:35
  67.8 5.7 %collective-permute-start.22 = (f32[16,512]{1,0:T(8,128)S(1)}, f32[16,512]{1,0:T(8,128)S(1)}, u32[]{:S(2)}, u32[]{:S(2)}) collective-permute-start(f32[16,512]{1,0:T(8,128)S(1)} %multiply_add_fusion.1.refs_4_), channel_id=1, source_target_pairs={{0,3},{1,2},{2,1},{3,0},{4,7},{5,6},{6,5},{7,4},{8,11},{9,10},{10,... | collective-permute-start | bytes 98312 | tf_op jit(solution)/shard_map/ppermute | solution.py:35
  78.4 7.6 %collective-permute-start.23 = (f32[16,512]{1,0:T(8,128)S(1)}, f32[16,512]{1,0:T(8,128)S(1)}, u32[]{:S(2)}, u32[]{:S(2)}) collective-permute-start(f32[16,512]{1,0:T(8,128)S(1)} %column_step.4.refs_4_.refs_8_), channel_id=1, source_target_pairs={{0,8},{4,12},{8,0},{12,4},{16,24},{20,28},{24,16},{28,20},{1,9},{5... | collective-permute-start | bytes 98312 | tf_op jit(solution)/shard_map/ppermute | solution.py:35
  78.5 9.4 %collective-permute-start.24 = (f32[16,512]{1,0:T(8,128)S(1)}, f32[16,512]{1,0:T(8,128)S(1)}, u32[]{:S(2)}, u32[]{:S(2)}) collective-permute-start(f32[16,512]{1,0:T(8,128)S(1)} %column_step.4.refs_4_.refs_8_), channel_id=1, source_target_pairs={{0,16},{4,20},{8,24},{12,28},{16,0},{20,4},{24,8},{28,12},{1,17},{... | collective-permute-start | bytes 98312 | tf_op jit(solution)/shard_map/ppermute | solution.py:35
  97.1 6.5 %collective-permute-start.29 = (f32[16,512]{1,0:T(8,128)S(1)}, f32[16,512]{1,0:T(8,128)S(1)}, u32[]{:S(2)}, u32[]{:S(2)}) collective-permute-start(f32[16,512]{1,0:T(8,128)S(1)} %multiply_add_fusion.refs_4_), channel_id=1, source_target_pairs={{0,3},{1,2},{2,1},{3,0},{4,7},{5,6},{6,5},{7,4},{8,11},{9,10},{10,... | collective-permute-start | bytes 98312 | tf_op jit(solution)/shard_map/ppermute | solution.py:35
  108.8 5.3 %collective-permute-start.32 = (f32[16,512]{1,0:T(8,128)S(1)}, f32[16,512]{1,0:T(8,128)S(1)}, u32[]{:S(2)}, u32[]{:S(2)}) collective-permute-start(f32[16,512]{1,0:T(8,128)S(1)} %column_step.5.refs_4_), channel_id=1, source_target_pairs={{0,24},{4,28},{8,16},{12,20},{16,8},{20,12},{24,0},{28,4},{1,25},{... | collective-permute-start | bytes 98312 | tf_op jit(solution)/shard_map/ppermute | solution.py:35
  119.0 5.6 %collective-permute-start.37 = (f32[16,512]{1,0:T(8,128)S(1)}, f32[16,512]{1,0:T(8,128)S(1)}, u32[]{:S(2)}, u32[]{:S(2)}) collective-permute-start(f32[16,512]{1,0:T(8,128)S(1)} %multiply_subtract_fusion), channel_id=1, source_target_pairs={{0,4},{4,0},{8,12},{12,8},{16,20},{20,16},{24,28},{28,24},{1,5},{5... | collective-permute-start | bytes 98312 | tf_op jit(solution)/shard_map/ppermute | solution.py:35
  120.2 5.3 %collective-permute-start.34 = (f32[8,512]{1,0:T(8,128)S(1)}, f32[8,512]{1,0:T(8,128)S(1)}, u32[]{:S(2)}, u32[]{:S(2)}) collective-permute-start(f32[8,512]{1,0:T(8,128)S(1)} %multiply_add_fusion.2.refs_0_), channel_id=1, source_target_pairs={{0,1},{1,0},{2,3},{3,2},{4,5},{5,4},{6,7},{7,6},{8,9},{9,8},{10,11... | collective-permute-start | bytes 49160 | tf_op jit(solution)/shard_map/ppermute | solution.py:35
  120.3 5.2 %collective-permute-start.35 = (f32[8,512]{1,0:T(8,128)S(1)}, f32[8,512]{1,0:T(8,128)S(1)}, u32[]{:S(2)}, u32[]{:S(2)}) collective-permute-start(f32[8,512]{1,0:T(8,128)S(1)} %multiply_add_fusion.2.refs_0_), channel_id=1, source_target_pairs={{0,2},{1,3},{2,0},{3,1},{4,6},{5,7},{6,4},{7,5},{8,10},{9,11},{10,... | collective-permute-start | bytes 49160 | tf_op jit(solution)/shard_map/ppermute | solution.py:35
  122.8 5.5 %collective-permute-start.36 = (f32[8,512]{1,0:T(8,128)S(1)}, f32[8,512]{1,0:T(8,128)S(1)}, u32[]{:S(2)}, u32[]{:S(2)}) collective-permute-start(f32[8,512]{1,0:T(8,128)S(1)} %multiply_add_fusion.2.refs_0_), channel_id=1, source_target_pairs={{0,3},{1,2},{2,1},{3,0},{4,7},{5,6},{6,5},{7,4},{8,11},{9,10},{10,... | collective-permute-start | bytes 49160 | tf_op jit(solution)/shard_map/ppermute | solution.py:35
  (18 other events, 56.7 us)
